TPU v7x, 32 devices: a whole 2x2x4 slice. The times are simulated.
32 devices in a mesh: ta: 2 (over x), gx: 16 (over z, y, core).
Axes of the slice: x: 2, y: 2, z: 4, core: 2. Of those that a mesh axis runs over, the one named last changes fastest.
Arguments:
- voltages: bfloat16 [2, 128, 2, 256, 512], P('ta', 'gx'), may hold values from -6 to 6
- weights: bfloat16 [2, 256, 2, 512, 64], P(None, 'gx'), may hold values from -0.125 to 0.125
Outputs:
- spectra: float32 [256, 2, 512, 64], P(None, None, 'gx', 'ta')
All inputs are finite; a program needn't handle non-finite values.
Results may differ from a plain program's by a relative error of at most 0.0003.
Values may be sent and summed in bfloat16 or wider, within the bound.
No kernel may reach another device: no remote copies, remote signals or barrier semaphores. Data moves between devices by JAX's collectives and lax.ppermute only.
A program may use at most 64 MiB of HBM per device.

v0:
```python
import jax
import jax.numpy as jnp
from jax import lax
from jax.sharding import PartitionSpec as P


def beam_power(voltage, weight_block):
    antennas = weight_block.shape[3]
    beam_count = weight_block.shape[2]
    powers = []
    for side_index in range(2):
        real_w = weight_block[side_index, 0]
        imag_w = weight_block[side_index, 1]
        upper_rows = jnp.stack([real_w, -imag_w], axis=-1).reshape(beam_count, 2 * antennas)
        bottom_half_rows = jnp.stack([imag_w, real_w], axis=-1).reshape(beam_count, 2 * antennas)
        matrix = jnp.concatenate([upper_rows, bottom_half_rows], 0)
        signal = voltage[side_index * antennas : (side_index + 1) * antennas].reshape(
            2 * antennas, -1
        )
        beam_voltage_field = jnp.dot(matrix, signal, preferred_element_type=jnp.float32)
        power = (
            beam_voltage_field[:beam_count] * beam_voltage_field[:beam_count]
            + beam_voltage_field[beam_count:] * beam_voltage_field[beam_count:]
        )
        powers.append(power.reshape(beam_count, -1, 8).sum(-1))
    return jnp.stack(powers, 0)


def channel_powers(turned, weights):

    def one_channel(column):
        voltage = lax.dynamic_index_in_dim(turned, column, 2, keepdims=False)
        weight_block = lax.dynamic_index_in_dim(weights, column, 1, keepdims=False)
        return beam_power(voltage, weight_block)

    return lax.map(one_channel, jnp.arange(turned.shape[2], dtype=jnp.int32))


def on_device(voltages, weights):
    turned = lax.all_to_all(voltages, "gx", split_axis=3, concat_axis=1, tiled=True)
    partial_power_value = channel_powers(turned[0], weights)
    relaid = lax.all_to_all(partial_power_value, "gx", split_axis=2, concat_axis=0, tiled=True)
    return lax.psum_scatter(relaid, "ta", scatter_dimension=3, tiled=True)


def solution(mesh):
    in_specs = (P("ta", "gx", None, None, None), P(None, "gx", None, None, None))
    out_specs = P(None, None, "gx", "ta")
    return jax.shard_map(
        on_device, mesh=mesh, in_specs=in_specs, out_specs=out_specs, check_vma=False
    )
```

profile of v0, /device:TPU:0, one launch (start us, length us, event | category | flops | bytes accessed | tf_op | source)
XLA Modules:
  0.0 490.1 jit_solution(4160567813515500975)
XLA Ops:
  6.5 6.5 %copy.34 = bf16[1,8,2,256,512]{4,1,2,0,3:T(8,128)(2,1)} copy(bf16[1,8,2,256,512]{4,3,2,1,0:T(8,128)(2,1)} %param.4) | data formatting | bytes 8388608 | tf_op args[0]
  13.0 7.5 %all-to-all-start = ((bf16[1,8,2,256,512]{4,1,2,0,3:T(8,128)(2,1)}), bf16[1,8,2,256,512]{4,1,2,0,3:T(8,128)(2,1)}, u32[]{:S(2)}, u32[]{:S(2)}) async-start(bf16[1,8,2,256,512]{4,1,2,0,3:T(8,128)(2,1)} %copy.34), calls=%async_computation | async-start | bytes 8388608 | tf_op jit(solution)/shard_map/all_to_all | solution.py:40
  20.5 77.5 %all-to-all-done = bf16[1,8,2,256,512]{4,1,2,0,3:T(8,128)(2,1)} async-done(((bf16[1,8,2,256,512]{4,1,2,0,3:T(8,128)(2,1)}), bf16[1,8,2,256,512]{4,1,2,0,3:T(8,128)(2,1)}, u32[]{:S(2)}, u32[]{:S(2)}) %all-to-all-start) | async-done | bytes 4194336 | tf_op jit(solution)/shard_map/all_to_all | solution.py:40
  98.0 8.5 %copy.35 = bf16[1,16,8,2,16,512]{5,3,2,1,4,0:T(2,128)(2,1)} copy(bf16[1,16,8,2,16,512]{5,2,3,4,1,0:T(8,128)(2,1)} %bitcast.12) | data formatting | bytes 8388608 | tf_op jit(solution)/shard_map/all_to_all | solution.py:40
  106.6 132.5 %while.10 = (s32[]{:T(128)}, f32[16,2,512,64]{2,3,1,0:T(8,128)}, s32[16]{0:T(128)S(1)}, bf16[2,16,2,512,64]{3,4,2,1,0:T(8,128)(2,1)}, bf16[128,2,16,512]{3,1,0,2...) while((s32[]{:T(128)}, f32[16,2,512,64]{2,3,1,0:T(8,128)}, s32[16]{0:T(128)S(1)}, ...), condition=%wide.region_3.4_spmd, body=%wide.region_0.3_spmd.sunk | while | flops 271908864 | bytes 15335599 | solution.py:36
  109.0 1.2 constant_dynamic-slice_fusion.3
  110.3 1.0 dynamic-slice_bitcast_fusion.2
  117.3 1.2 constant_dynamic-slice_fusion.3
  118.6 1.0 dynamic-slice_bitcast_fusion.2
  125.6 1.2 constant_dynamic-slice_fusion.3
  126.8 1.0 dynamic-slice_bitcast_fusion.2
  130.7 0.7 fusion.40
  133.9 1.2 constant_dynamic-slice_fusion.3
  135.1 1.0 dynamic-slice_bitcast_fusion.2
  139.0 0.7 fusion.40
  142.2 1.2 constant_dynamic-slice_fusion.3
  143.4 1.0 dynamic-slice_bitcast_fusion.2
  150.4 1.2 constant_dynamic-slice_fusion.3
  151.7 1.0 dynamic-slice_bitcast_fusion.2
  158.7 1.2 constant_dynamic-slice_fusion.3
  160.0 1.0 dynamic-slice_bitcast_fusion.2
  167.0 1.2 constant_dynamic-slice_fusion.3
  168.3 1.0 dynamic-slice_bitcast_fusion.2
  175.3 1.2 constant_dynamic-slice_fusion.3
  176.6 1.0 dynamic-slice_bitcast_fusion.2
  183.6 1.2 constant_dynamic-slice_fusion.3
  184.9 1.0 dynamic-slice_bitcast_fusion.2
  191.9 1.2 constant_dynamic-slice_fusion.3
  193.2 1.0 dynamic-slice_bitcast_fusion.2
  200.2 1.2 constant_dynamic-slice_fusion.3
  201.4 1.0 dynamic-slice_bitcast_fusion.2
  208.4 1.2 constant_dynamic-slice_fusion.3
  209.7 1.0 dynamic-slice_bitcast_fusion.2
  216.7 1.2 constant_dynamic-slice_fusion.3
  218.0 1.0 dynamic-slice_bitcast_fusion.2
  225.0 1.2 constant_dynamic-slice_fusion.3
  226.3 1.0 dynamic-slice_bitcast_fusion.2
  233.2 1.2 constant_dynamic-slice_fusion.3
  234.5 1.0 dynamic-slice_bitcast_fusion.2
  239.1 12.2 %copy.37 = f32[16,2,512,64]{3,1,0,2:T(2,128)} copy(f32[16,2,512,64]{2,3,1,0:T(8,128)} %get-tuple-element.32) | data formatting | bytes 8388608 | tf_op jit(solution)/shard_map/while | solution.py:36
  251.3 15.1 %reshape.49 = f32[16,1,65536]{2,1,0:T(1,128)} reshape(f32[512,16,2,64]{3,2,1,0:T(2,128)} %bitcast.77) | data formatting | bytes 8388608
  266.4 111.8 %all_to_all.33 = f32[16,1,65536]{2,1,0:T(1,128)} all-to-all(f32[16,1,65536]{2,1,0:T(1,128)} %reshape.49), channel_id=1, replica_groups=mesh['ta'=2,'gx'=16] {'gx'}, dimensions={0} | all-to-all | bytes 8388608 | tf_op jit(solution)/shard_map/all_to_all | solution.py:42
  378.8 13.7 %reduce = f32[16,65536]{1,0:T(8,128)} reduce(f32[16,1,65536]{2,1,0:T(1,128)} %all_to_all.33, f32[]{:T(128)} %broadcast), dimensions={1}, to_apply=%all_to_all.27.reduce_sub_computation | reduce | bytes 8388612 | tf_op jit(solution)/shard_map/all_to_all | solution.py:42
  392.5 9.7 %reshape.50 = f32[512,16,2,64]{3,2,1,0:T(2,128)} reshape(f32[16,65536]{1,0:T(8,128)} %reduce) | data formatting | bytes 8388608
  402.2 13.1 %copy.38 = f32[16,2,16,32,64]{4,3,1,0,2:T(8,128)} copy(f32[16,2,16,32,64]{4,1,0,3,2:T(2,128)} %bitcast.78) | data formatting | bytes 8388608 | tf_op jit(solution)/shard_map/all_to_all | solution.py:42
  415.2 8.7 %copy.39 = f32[256,2,32,64]{0,2,1,3:T(8,128)} copy(f32[256,2,32,64]{3,2,1,0:T(8,128)} %bitcast.79) | data formatting | bytes 8388608 | tf_op jit(solution)/shard_map/all_to_all | solution.py:42
  423.9 55.2 %reduce-scatter.2.cloned.1.call-done = f32[256,2,32,32]{0,2,1,3:T(8,128)} async-done(((f32[256,2,32,64]{0,2,1,3:T(8,128)}), f32[256,2,32,32]{0,2,1,3:T(8,128)}) %reduce-scatter.2.cloned.1.call-update) | async-done | bytes 2097168 | tf_op jit(solution)/shard_map/reduce_scatter | solution.py:43
  479.1 4.1 copy.40
  (307 shorter events, 65.9 us)
Async XLA Ops:
  13.0 85.0 %all-to-all-start = ((bf16[1,8,2,256,512]{4,1,2,0,3:T(8,128)(2,1)}), bf16[1,8,2,256,512]{4,1,2,0,3:T(8,128)(2,1)}, u32[]{:S(2)}, u32[]{:S(2)}) async-start(bf16[1,8,2,256,512]{4,1,2,0,3:T(8,128)(2,1)} %copy.34), calls=%async_computation | async-start | bytes 8388608 | tf_op jit(solution)/shard_map/all_to_all | solution.py:40
  20.5 458.7 %reduce-scatter.2.cloned.1.call-start = ((), (), s32[]{:S(2)}) async-start(), calls=%async_computation.3 | async-start | bytes 6291456 | tf_op jit(solution)/shard_map/reduce_scatter | solution.py:43
Sparse Core Ops, SparseCore 0:
  424.0 55.0 reduce-scatter.1
where the time goes:
time: 492 us; the launch traced here: 490 us
  local copies, waits for them, and re-layouts  137 us (28%)
  waiting for transfers between devices  133 us (27%)
  blocking collectives  112 us (23%)
  other arithmetic  41.3 us (8%)
  loops' own time  31.5 us (6%)
  matrix products  15.2 us (3%)
  between operations  13.4 us (3%)
  starting transfers between devices  7.51 us (2%)
    all_to_all x1, blocking collectives, on_device(): lax.all_to_all(partial_power_value, 'gx', split_axis=2, concat_axis=0, ti...  112 us
    all_to_all x1, waiting for transfers between devices, on_device(): lax.all_to_all(voltages, 'gx', split_axis=3, concat_axis=1, tiled=True)  77.5 us
    reduce_scatter x1, waiting for transfers between devices, on_device(): return lax.psum_scatter(relaid, 'ta', scatter_dimension=3, tiled=True)  55.2 us
    another operation x1, loops' own time, channel_powers(): return lax.map(one_channel, jnp.arange(turned.shape[2], dtype=jnp.int32))  31.5 us
    unnamed x3, local copies, waits for them, and re-layouts  31.2 us
    all_to_all x3, local copies, waits for them, and re-layouts, on_device(): lax.all_to_all(partial_power_value, 'gx', split_axis=2, concat_axis=0, ti...  22.2 us
    slice x16, local copies, waits for them, and re-layouts, beam_power(): voltage[side_index * antennas:(side_index + 1) * antennas]  18.5 us
    squeeze x16, local copies, waits for them, and re-layouts, one_channel(): weight_block = lax.dynamic_index_in_dim(weights, column, 1, keepdims=False)  15.6 us
  transfers between devices with their start and end apart: 2, of which 2 were waited for; matrix products, arithmetic and copies ran while one was open for 0% of the time, Pallas kernels for 0%

commit v1 on v0

v1 whole, which is shorter than its diff:
```python
import functools

import jax
import jax.numpy as jnp
from jax import lax
from jax.experimental import pallas as pl
from jax.experimental.pallas import tpu as pltpu
from jax.sharding import Mesh, PartitionSpec as P

BIN = 8
LANES = 128
AXES = ("ta", "gh", "gl")


def beam_kernel(dims, x_ref, w_ref, o_ref, xf, xt, xb):
    halves, locals_, streams, channels, samples, beams, groups = dims
    antennas = locals_ * streams
    bins = samples // BIN
    owned = beams // groups
    stack = LANES // owned
    own_bins = bins // halves
    rows = own_bins // stack
    tile = 256
    block = 256

    def widen(source, carry):
        for chunk in range(0, samples, LANES):
            xf[source, chunk // LANES] = x_ref[source, :, chunk : chunk + LANES].astype(
                jnp.float32
            )
        return carry

    lax.fori_loop(0, halves * locals_, widen, 0)

    def one_channel(channel, carry):
        for half in range(halves):
            for chunk in range(0, samples, LANES):
                parts = []
                for part in range(2):
                    for local in range(locals_):
                        rows_of = pl.ds(part * channels + channel, streams, stride=2 * channels)
                        parts.append(xf[half * locals_ + local, chunk // LANES, rows_of, :])
                xt[half, chunk : chunk + LANES, :] = jnp.concatenate(parts, axis=0).T
        for half in range(halves):
            for index in range(BIN):
                base = (half * BIN + index) * bins
                xb[base : base + bins, :] = xt[half, pl.ds(index, bins, stride=BIN), :].astype(
                    jnp.bfloat16
                )
        w_re = w_ref[channel, 0]
        w_im = w_ref[channel, 1]
        for column in range(0, beams, tile):
            a = w_re[:, column : column + tile]
            b = w_im[:, column : column + tile]
            for_re = jnp.concatenate([a, -b], axis=0)
            for_im = jnp.concatenate([b, a], axis=0)
            total = jnp.zeros((bins, tile), jnp.float32)
            for base in range(0, halves * samples, block):
                lhs = xb[base : base + block, :]
                re = jnp.dot(lhs, for_re, preferred_element_type=jnp.float32)
                im = jnp.dot(lhs, for_im, preferred_element_type=jnp.float32)
                power = re * re + im * im
                for piece in range(0, block, bins):
                    total = total + power[piece : piece + bins]
            lane = lax.broadcasted_iota(jnp.int32, (rows, LANES), 1) // owned
            for group in range(0, tile, LANES):
                for half in range(halves):
                    parts = [
                        total[
                            half * own_bins + k * rows : half * own_bins + (k + 1) * rows,
                            group : group + LANES,
                        ]
                        for k in range(stack)
                    ]
                    for dest in range(stack):
                        out = None
                        for k in range(stack):
                            turn = ((k - dest) * owned) % LANES
                            moved = parts[k] if turn == 0 else pltpu.roll(parts[k], turn, 1)
                            out = moved if out is None else jnp.where(lane == k, moved, out)
                        number = half * groups + (column + group) // owned + dest
                        o_ref[number, channel] = out
        return carry

    lax.fori_loop(0, channels, one_channel, 0)


def form_beams(x, w, halves, groups):
    sources, streams, _, channels, samples = x.shape
    beams = w.shape[3]
    locals_ = sources // halves
    bins = samples // BIN
    owned = beams // groups
    rows = bins // halves * owned // LANES
    antennas = locals_ * streams
    dims = (halves, locals_, streams, channels, samples, beams, groups)
    flops = 2 * channels * halves * samples * 2 * beams * 2 * antennas
    vmem = pl.BlockSpec(memory_space=pltpu.VMEM)
    return pl.pallas_call(
        functools.partial(beam_kernel, dims),
        out_shape=jax.ShapeDtypeStruct((halves * groups, channels, rows, LANES), jnp.float32),
        in_specs=[vmem, vmem],
        out_specs=vmem,
        scratch_shapes=[
            pltpu.VMEM((sources, samples // LANES, streams * 2 * channels, LANES), jnp.float32),
            pltpu.VMEM((halves, samples, 2 * antennas), jnp.float32),
            pltpu.VMEM((halves * samples, 2 * antennas), jnp.bfloat16),
        ],
        compiler_params=pltpu.CompilerParams(vmem_limit_bytes=40 << 20),
        cost_estimate=pl.CostEstimate(flops=flops, bytes_accessed=4 << 20, transcendentals=0),
        name="form_beams",
    )(x.reshape(sources, streams * 2 * channels, samples), w)


def gather_kernel(dims, own_ref, other_ref, o_ref, turned_ref):
    halves, locals_, channels, rows, owned = dims
    stack = LANES // owned
    for side in range(2):
        for row in range(rows):
            parts = []
            for block in range(2):
                ref = own_ref if block == side else other_ref
                for local in range(locals_):
                    for half in range(halves):
                        source = (half * 2 + side) * locals_ + local
                        parts.append(ref[source, pl.ds(row, channels, stride=rows), :])
            table = jnp.concatenate(parts, axis=0)
            for column in range(0, table.shape[0], LANES):
                turned = table[column : column + LANES].T
                for k in range(stack):
                    places = pl.ds(k * rows + row, owned, stride=stack * rows)
                    turned_ref[column // LANES, places, :] = turned[k * owned : (k + 1) * owned]
        for column in range(turned_ref.shape[0]):
            o_ref[side, :, column * LANES : (column + 1) * LANES] = turned_ref[column]


def gather_spectra(own, other, halves, owned):
    sources, channels, rows, _ = own.shape
    locals_ = sources // (2 * halves)
    dims = (halves, locals_, channels, rows, owned)
    count = 2 * locals_ * halves * channels
    bins = rows * LANES // owned
    vmem = pl.BlockSpec(memory_space=pltpu.VMEM)
    out = pl.pallas_call(
        functools.partial(gather_kernel, dims),
        out_shape=jax.ShapeDtypeStruct((2, owned * bins, count), jnp.float32),
        in_specs=[vmem, vmem],
        out_specs=vmem,
        scratch_shapes=[pltpu.VMEM((count // LANES, owned * bins, LANES), jnp.float32)],
        compiler_params=pltpu.CompilerParams(vmem_limit_bytes=40 << 20),
        name="gather_spectra",
    )(
        own.reshape(sources, channels * rows, LANES),
        other.reshape(sources, channels * rows, LANES),
    )
    return out.reshape(2, owned, bins, count).transpose(3, 0, 1, 2)


def plain_beams(x, w, halves, groups):
    sources, streams, _, channels, samples = x.shape
    beams = w.shape[3]
    antennas = sources // halves * streams
    v = x.reshape(halves, antennas, 2, channels, samples)
    args = dict(preferred_element_type=jnp.float32)
    rr = jnp.einsum("jab,hajs->hjbs", w[:, 0], v[:, :, 0], **args)
    ii = jnp.einsum("jab,hajs->hjbs", w[:, 1], v[:, :, 1], **args)
    ri = jnp.einsum("jab,hajs->hjbs", w[:, 0], v[:, :, 1], **args)
    ir = jnp.einsum("jab,hajs->hjbs", w[:, 1], v[:, :, 0], **args)
    re, im = rr - ii, ri + ir
    power = (re * re + im * im).reshape(halves, channels, beams, samples // BIN, BIN)
    total = power.sum((0, 4)).reshape(channels, groups, beams // groups, halves, -1)
    return total.transpose(3, 1, 0, 2, 4).reshape(
        halves * groups, channels, beams // groups, samples // BIN // halves
    )


def plain_gather(own, other, halves, owned):
    sources, channels, _, bins = own.shape
    locals_ = sources // (2 * halves)
    sides = []
    for side in range(2):
        blocks = []
        for block in range(2):
            part = (own if block == side else other).reshape(
                halves, 2, locals_, channels, owned, bins
            )[:, side]
            blocks.append(part.transpose(1, 0, 2, 3, 4))
        sides.append(jnp.stack(blocks).reshape(-1, owned, bins))
    return jnp.stack(sides, 1)


def on_device(halves, groups, voltages, weights):
    _, streams, _, channel_total, samples = voltages.shape
    locals_ = groups // 2
    part = channel_total // (groups * halves)
    beams = weights.shape[3]
    owned = beams // groups
    tiled = (
        LANES % owned == 0
        and samples // BIN // halves * owned == 8 * LANES
        and streams == 8
        and part == 8
        and beams % 256 == 0
    )
    side = lax.axis_index("gh")
    half = lax.axis_index("ta")

    w = weights.reshape((2, halves, part) + weights.shape[2:])
    w = lax.dynamic_index_in_dim(w, half, 1, keepdims=False).transpose(0, 1, 2, 4, 3)
    w_own = lax.dynamic_index_in_dim(w, side, 0, keepdims=False)
    w_sent = lax.dynamic_index_in_dim(w, 1 - side, 0, keepdims=False)
    w_other = lax.ppermute(w_sent, "gh", [(0, 1), (1, 0)])

    v = voltages.reshape(streams, 2, 2, locals_, halves, part, samples)
    moved = []
    for block in range(2):
        piece = lax.dynamic_index_in_dim(v, side ^ block, 2, keepdims=False)
        piece = piece.transpose(3, 2, 0, 1, 4, 5).reshape(
            halves * locals_, streams, 2, part, samples
        )
        moved.append(lax.all_to_all(piece, ("ta", "gl"), 0, 0, tiled=True))
    form = form_beams if tiled else plain_beams
    gather = gather_spectra if tiled else plain_gather
    spectra = []
    for block in range(2):
        pieces = form(moved[block], w_own if block == 0 else w_other, halves, groups)
        spectra.append(lax.all_to_all(pieces, AXES, 0, 0, tiled=True))
    return gather(spectra[0], spectra[1], halves, owned)


def solution(mesh):
    halves, groups = mesh.shape["ta"], mesh.shape["gx"]
    cut = Mesh(mesh.devices.reshape(halves, 2, groups // 2), AXES)
    in_specs = (
        P("ta", ("gh", "gl"), None, None, None),
        P(None, ("gh", "gl"), None, None, None),
    )
    out_specs = P(None, None, ("gh", "gl"), "ta")
    return jax.shard_map(
        functools.partial(on_device, halves, groups),
        mesh=cut,
        in_specs=in_specs,
        out_specs=out_specs,
        check_vma=False,
    )
```

time: 492 us -> 193 us (0.39)
  local copies, waits for them, and re-layouts: 137 us -> 15.1 us
  blocking collectives: 112 us -> 30.7 us
  other arithmetic: 41.3 us -> 0 us
  loops' own time: 31.5 us -> 0 us
  waiting for transfers between devices: 133 us -> 110 us
  Pallas kernels: 0 us -> 20.4 us
  matrix products: 15.2 us -> 0 us
  between operations: 13.4 us -> 0.09 us
  starting transfers between devices: 7.51 us -> 16.1 us
    all_to_all x1, blocking collectives: 112 us -> 30.7 us  [on_device(): spectra.append(lax.all_to_all(pieces, AXES, 0, 0, tiled=True))]
    ppermute x0 -> x1, waiting for transfers between devices: none -> 68.5 us  [on_device(): w_other = lax.ppermute(w_sent, 'gh', [(0, 1), (1, 0)])]
    reduce_scatter x1 -> x0, waiting for transfers between devices: 55.2 us -> none  [on_device(): return lax.psum_scatter(relaid, 'ta', scatter_dimension=3, tiled=True)]
    all_to_all x1 -> x3, waiting for transfers between devices: 77.5 us -> 41.8 us  [the longest x2 41.8 us: on_device(): moved.append(lax.all_to_all(piece, ('ta', 'gl'), 0, 0, tiled=True))]
    another operation x1 -> x0, loops' own time: 31.5 us -> none  [channel_powers(): return lax.map(one_channel, jnp.arange(turned.shape[2], dtype=jnp.int32))]
    all_to_all x4 -> x0, local copies, waits for them, and re-layouts: 30.8 us -> none  [the longest x3 22.2 us: on_device(): lax.all_to_all(partial_power_value, 'gx', split_axis=2, concat_axis=0, ti...]
    unnamed x3 -> x8, local copies, waits for them, and re-layouts: 31.2 us -> 3.26 us
    pallas_call x0 -> x3, Pallas kernels: none -> 20.4 us  [the longest x2 16.7 us: form_beams(): pl.pallas_call(functools.partial(beam_kernel, dims), out_shape=jax.ShapeD...]
  transfers between devices with their start and end apart: 2 -> 4, of which waited for: 2 -> 3; matrix products, arithmetic and copies ran while one was open for 0% -> 3% of each run, Pallas kernels for 0% -> 9%
where the time goes in v1:
time: 193 us
  waiting for transfers between devices  110 us (57%)
  blocking collectives  30.7 us (16%)
  Pallas kernels  20.4 us (11%)
  starting transfers between devices  16.1 us (8%)
  local copies, waits for them, and re-layouts  15.1 us (8%)
    ppermute x1, waiting for transfers between devices, on_device(): w_other = lax.ppermute(w_sent, 'gh', [(0, 1), (1, 0)])  68.5 us
    all_to_all x2, waiting for transfers between devices, on_device(): moved.append(lax.all_to_all(piece, ('ta', 'gl'), 0, 0, tiled=True))  41.8 us
    all_to_all x1, blocking collectives, on_device(): spectra.append(lax.all_to_all(pieces, AXES, 0, 0, tiled=True))  30.7 us
    pallas_call x2, Pallas kernels, form_beams(): pl.pallas_call(functools.partial(beam_kernel, dims), out_shape=jax.ShapeD...  16.7 us
    all_to_all x2, starting transfers between devices, on_device(): moved.append(lax.all_to_all(piece, ('ta', 'gl'), 0, 0, tiled=True))  10 us
    transpose x3, local copies, waits for them, and re-layouts, on_device(): piece.transpose(3, 2, 0, 1, 4, 5)  8.92 us
  transfers between devices with their start and end apart: 4, of which 3 were waited for; matrix products, arithmetic and copies ran while one was open for 3% of the time, Pallas kernels for 9%

profile of v1, /device:TPU:0, one launch (start us, length us, event | category | flops | bytes accessed | tf_op | source)
XLA Modules:
  0.0 192.7 jit_solution(15685481238944471341)
XLA Ops:
  0.0 4.1 %dynamic-slice_bitcast_fusion = (bf16[2,8,8,2,8,512]{5,4,0,1,3,2:T(8,128)(2,1)}, bf16[2,8,8,2,8,512]{5,4,0,1,3,2:T(8,128)(2,1)S(1)}) fusion(bf16[8,2,2,8,2,8,512]{6,5,4,3,2,1,0:T(8,128)(2,1)} %bitcast.37, s32[]{:T(128)S(6)} %select_n.26, s32[]{:T(128)S(6)} %select_n.22), kind=kLoop, calls=%fused_computation | loop fusion | bytes 8388616 | tf_op jit(solution)/shard_map/transpose | solution.py:218
  4.1 1.6 copy.3
  5.7 6.3 %all-to-all-start = ((bf16[16,8,2,8,512]{4,3,2,1,0:T(8,128)(2,1)}), bf16[16,8,2,8,512]{4,3,2,1,0:T(8,128)(2,1)S(1)}, u32[]{:S(2)}, u32[]{:S(2)}) async-start(bf16[16,8,2,8,512]{4,3,2,1,0:T(8,128)(2,1)} %bitcast.36), calls=%async_computation | async-start | bytes 4194304 | tf_op jit(solution)/shard_map/all_to_all | solution.py:221
  12.0 3.2 %copy.4 = bf16[2,8,8,2,8,512]{5,4,3,2,1,0:T(8,128)(2,1)} copy(bf16[2,8,8,2,8,512]{5,4,0,1,3,2:T(8,128)(2,1)} %get-tuple-element.7) | data formatting | bytes 4194304 | tf_op jit(solution)/shard_map/transpose | solution.py:218
  15.2 25.4 %all-to-all-done = bf16[16,8,2,8,512]{4,3,2,1,0:T(8,128)(2,1)S(1)} async-done(((bf16[16,8,2,8,512]{4,3,2,1,0:T(8,128)(2,1)}), bf16[16,8,2,8,512]{4,3,2,1,0:T(8,128)(2,1)S(1)}, u32[]{:S(2)}, u32[]{:S(2)}) %all-to-all-start) | async-done | bytes 2097184 | tf_op jit(solution)/shard_map/all_to_all | solution.py:221
  40.6 0.0 copy-start
  40.6 1.3 copy-done
  42.0 3.7 %all-to-all-start.2 = ((bf16[16,8,2,8,512]{4,3,2,1,0:T(8,128)(2,1)}), bf16[16,8,2,8,512]{4,3,2,1,0:T(8,128)(2,1)S(1)}, u32[]{:S(2)}, u32[]{:S(2)}) async-start(bf16[16,8,2,8,512]{4,3,2,1,0:T(8,128)(2,1)} %bitcast.35), calls=%async_computation.2 | async-start | bytes 4194304 | tf_op jit(solution)/shard_map/all_to_all | solution.py:221
  45.7 0.0 copy-start.1
  45.7 2.9 %dynamic-slice_bitcast_fusion.2 = (bf16[8,2,64,512]{3,2,1,0:T(8,128)(2,1)}, bf16[8,2,64,512]{3,2,1,0:T(8,128)(2,1)S(1)}) fusion(bf16[2,2,8,2,512,64]{4,5,3,2,1,0:T(8,128)(2,1)} %bitcast.38, s32[]{:T(128)S(6)} %select_n.28, s32[]{:T(128)S(6)} %select_n.25, s32[]{:T(128)S(6)} %select_n.23), kind=kLoop, calls=%fused_computation.2 | loop fusion | bytes 4194316 | tf_op jit(solution)/shard_map/jit(dynamic_index_in_dim)/squeeze | solution.py:211
  48.6 0.0 copy-done.1
  48.6 8.3 %form_beams.2 = f32[32,8,8,128]{3,2,1,0:T(8,128)S(1)} custom-call(bf16[16,128,512]{2,1,0:T(8,128)(2,1)S(1)} %bitcast.34, bf16[8,2,64,512]{3,2,1,0:T(8,128)(2,1)S(1)} %get-tuple-element.6.w_ref), custom_call_target="tpu_custom_call" | custom-call | flops 2147483648 | bytes 4194304 | tf_op jit(solution)/shard_map/form_beams/pallas_call | solution.py:99
  56.9 0.0 copy-start.2
  57.0 1.0 copy-done.2
  57.9 16.4 %all-to-all-done.2 = bf16[16,8,2,8,512]{4,3,2,1,0:T(8,128)(2,1)S(1)} async-done(((bf16[16,8,2,8,512]{4,3,2,1,0:T(8,128)(2,1)}), bf16[16,8,2,8,512]{4,3,2,1,0:T(8,128)(2,1)S(1)}, u32[]{:S(2)}, u32[]{:S(2)}) %all-to-all-start.2) | async-done | bytes 2097184 | tf_op jit(solution)/shard_map/all_to_all | solution.py:221
  74.3 3.3 %all-to-all-start.1 = ((f32[32,8,8,128]{3,2,1,0:T(8,128)}), f32[32,8,8,128]{3,2,1,0:T(8,128)S(1)}, u32[]{:S(2)}, u32[]{:S(2)}) async-start(f32[32,8,8,128]{3,2,1,0:T(8,128)} %copy-done.2), calls=%async_computation.1 | async-start | bytes 2097152 | tf_op jit(solution)/shard_map/all_to_all | solution.py:227
  77.6 2.7 %collective-permute-start = (bf16[8,2,64,512]{3,2,1,0:T(8,128)(2,1)}, bf16[8,2,64,512]{3,2,1,0:T(8,128)(2,1)S(1)}, u32[]{:S(2)}, u32[]{:S(2)}) collective-permute-start(bf16[8,2,64,512]{3,2,1,0:T(8,128)(2,1)} %get-tuple-element.5), channel_id=1, source_target_pairs={{0,8},{8,0},{1,9},{9,1},{2,10},{10,2},{3,11},{11,3},{4,12},{12,4},... | collective-permute-start | bytes 3145736 | tf_op jit(solution)/shard_map/ppermute | solution.py:212
  80.4 68.5 %collective-permute-done.w_ref = bf16[8,2,64,512]{3,2,1,0:T(8,128)(2,1)S(1)} collective-permute-done((bf16[8,2,64,512]{3,2,1,0:T(8,128)(2,1)}, bf16[8,2,64,512]{3,2,1,0:T(8,128)(2,1)S(1)}, u32[]{:S(2)}, u32[]{:S(2)}) %collective-permute-start) | collective-permute-done | bytes 1048608 | tf_op jit(solution)/shard_map/ppermute | solution.py:212
  148.8 8.3 %form_beams.3 = f32[32,8,8,128]{3,2,1,0:T(8,128)S(1)} custom-call(bf16[16,128,512]{2,1,0:T(8,128)(2,1)S(1)} %bitcast.33, bf16[8,2,64,512]{3,2,1,0:T(8,128)(2,1)S(1)} %collective-permute-done.w_ref), custom_call_target="tpu_custom_call" | custom-call | flops 2147483648 | bytes 4194304 | tf_op jit(solution)/shard_map/form_beams/pallas_call | solution.py:99
  157.2 0.0 copy-start.3
  157.2 1.0 copy-done.3
  158.1 0.0 all-to-all-done.1
  158.1 30.7 %all_to_all.20 = f32[32,8,8,128]{3,2,1,0:T(8,128)S(1)} all-to-all(f32[32,8,8,128]{3,2,1,0:T(8,128)} %copy-done.3), channel_id=1, replica_groups=mesh['ta'=2,'gh'=2,'gl'=8] {'ta','gh','gl'}, dimensions={0} | all-to-all | bytes 2097152 | tf_op jit(solution)/shard_map/all_to_all | solution.py:227
  188.9 3.8 %gather_spectra.1 = f32[2,1024,256]{2,1,0:T(8,128)} custom-call(f32[32,64,128]{2,1,0:T(8,128)S(1)} %bitcast.31, f32[32,64,128]{2,1,0:T(8,128)S(1)} %bitcast.32), custom_call_target="tpu_custom_call" | custom-call | tf_op jit(solution)/shard_map/gather_spectra/pallas_call | solution.py:144
Async XLA Ops:
  5.7 35.0 %all-to-all-start = ((bf16[16,8,2,8,512]{4,3,2,1,0:T(8,128)(2,1)}), bf16[16,8,2,8,512]{4,3,2,1,0:T(8,128)(2,1)S(1)}, u32[]{:S(2)}, u32[]{:S(2)}) async-start(bf16[16,8,2,8,512]{4,3,2,1,0:T(8,128)(2,1)} %bitcast.36), calls=%async_computation | async-start | bytes 4194304 | tf_op jit(solution)/shard_map/all_to_all | solution.py:221
  40.6 1.3 copy-start
  42.0 32.3 %all-to-all-start.2 = ((bf16[16,8,2,8,512]{4,3,2,1,0:T(8,128)(2,1)}), bf16[16,8,2,8,512]{4,3,2,1,0:T(8,128)(2,1)S(1)}, u32[]{:S(2)}, u32[]{:S(2)}) async-start(bf16[16,8,2,8,512]{4,3,2,1,0:T(8,128)(2,1)} %bitcast.35), calls=%async_computation.2 | async-start | bytes 4194304 | tf_op jit(solution)/shard_map/all_to_all | solution.py:221
  45.7 2.9 %copy-start.1 = (bf16[16,8,2,8,512]{4,3,2,1,0:T(8,128)(2,1)S(1)}, bf16[16,8,2,8,512]{4,3,2,1,0:T(8,128)(2,1)}, u32[]{:S(2)}) copy-start(bf16[16,8,2,8,512]{4,3,2,1,0:T(8,128)(2,1)} %copy-done) | copy-start | bytes 6291460
  56.9 1.0 copy-start.2
  74.3 83.8 %all-to-all-start.1 = ((f32[32,8,8,128]{3,2,1,0:T(8,128)}), f32[32,8,8,128]{3,2,1,0:T(8,128)S(1)}, u32[]{:S(2)}, u32[]{:S(2)}) async-start(f32[32,8,8,128]{3,2,1,0:T(8,128)} %copy-done.2), calls=%async_computation.1 | async-start | bytes 2097152 | tf_op jit(solution)/shard_map/all_to_all | solution.py:227
  77.6 71.2 %collective-permute-start = (bf16[8,2,64,512]{3,2,1,0:T(8,128)(2,1)}, bf16[8,2,64,512]{3,2,1,0:T(8,128)(2,1)S(1)}, u32[]{:S(2)}, u32[]{:S(2)}) collective-permute-start(bf16[8,2,64,512]{3,2,1,0:T(8,128)(2,1)} %get-tuple-element.5), channel_id=1, source_target_pairs={{0,8},{8,0},{1,9},{9,1},{2,10},{10,2},{3,11},{11,3},{4,12},{12,4},... | collective-permute-start | bytes 3145736 | tf_op jit(solution)/shard_map/ppermute | solution.py:212
  157.2 1.0 copy-start.3
